TPU v7x, 32 devices: a whole 2x2x4 slice. The times are simulated.
32 devices in a mesh: row: 4 (over z), col: 2 (over x), depth: 4 (over y, core).
Axes of the slice: x: 2, y: 2, z: 4, core: 2. Of those that a mesh axis runs over, the one named last changes fastest.
Arguments:
- pair_input: bfloat16 [192, 192, 128], P('row', ('col', 'depth')), may hold values from -40 to 40
- in_gain: float32 [128], replicated, may hold values from 0.1 to 1.9
- in_shift: float32 [128], replicated, may hold values from -3 to 3
- w_proj: bfloat16 [128, 512], replicated, may hold values from -0.5 to 0.5
- w_gate: bfloat16 [128, 128], replicated, may hold values from -0.5 to 0.5
- out_gain: float32 [128], replicated, may hold values from 0.1 to 1.9
- out_shift: float32 [128], replicated, may hold values from -3 to 3
- w_out: bfloat16 [128, 128], replicated, may hold values from -0.5 to 0.5
Outputs:
- update: bfloat16 [192, 192, 128], P('row', ('col', 'depth'))
All inputs are finite; a program needn't handle non-finite values.
Results may differ from a plain program's by a relative error of at most 0.013.
Values may be sent and summed in bfloat16 or wider, within the bound.
A program may use at most 64 MiB of HBM per device.

v0:
```python
import jax
import jax.numpy as jnp
from jax import lax
from jax.sharding import PartitionSpec as P


def layer_norm(values, scaling, offsets):
    average = jnp.mean(values, axis=-1, keepdims=True)
    centred = values - average
    variance = jnp.mean(centred * centred, axis=-1, keepdims=True)
    return centred * lax.rsqrt(variance + 1e-05) * scaling + offsets


def gated_sides(normed, w_proj):
    channels = w_proj.shape[1] // 4
    projected = jnp.einsum("xyc,cd->xyd", normed, w_proj, preferred_element_type=jnp.float32)
    left_side = (
        jax.nn.sigmoid(projected[..., :channels]) * projected[..., channels : 2 * channels]
    ).astype(jnp.bfloat16)
    right_side = (
        jax.nn.sigmoid(projected[..., 2 * channels : 3 * channels]) * projected[..., 3 * channels :]
    ).astype(jnp.bfloat16)
    return (left_side, right_side)


def reorder_channels(values, row_count, other_count):
    shape_rest = values.shape[1:]
    grouped = values.reshape((row_count, other_count, -1) + shape_rest)
    return jnp.swapaxes(grouped, 0, 1).reshape(values.shape)


def per_device(pair_input, in_gain, in_shift, w_proj, w_gate, out_gain, out_shift, w_out):
    row_count = lax.axis_size("row")
    col_count = lax.axis_size("col")
    depth_count = lax.axis_size("depth")
    normed = layer_norm(pair_input.astype(jnp.float32), in_gain, in_shift).astype(jnp.bfloat16)
    left_side, right_side = gated_sides(normed, w_proj)
    left_all, right_all = (
        lax.all_to_all(
            lax.all_to_all(left_side, "row", split_axis=2, concat_axis=0, tiled=True),
            ("col", "depth"),
            split_axis=2,
            concat_axis=1,
            tiled=True,
        ),
        lax.all_to_all(
            lax.all_to_all(right_side, "row", split_axis=2, concat_axis=0, tiled=True),
            ("col", "depth"),
            split_axis=2,
            concat_axis=1,
            tiled=True,
        ),
    )
    planes = jnp.einsum("kic,kjc->ijc", left_all, right_all, preferred_element_type=jnp.float32)
    product = lax.all_to_all(
        lax.all_to_all(planes.astype(jnp.bfloat16), "row", split_axis=0, concat_axis=2, tiled=True),
        ("col", "depth"),
        split_axis=1,
        concat_axis=2,
        tiled=True,
    ).astype(planes.dtype)
    other_count = col_count * depth_count
    used_gain = reorder_channels(out_gain, row_count, other_count)
    used_shift = reorder_channels(out_shift, row_count, other_count)
    used_out = reorder_channels(w_out, row_count, other_count)
    product_norm = layer_norm(product, used_gain, used_shift).astype(jnp.bfloat16)
    gating = jax.nn.sigmoid(
        jnp.einsum("xyc,cd->xyd", normed, w_gate, preferred_element_type=jnp.float32)
    )
    projected_out = jnp.einsum(
        "xyc,cd->xyd", product_norm, used_out, preferred_element_type=jnp.float32
    )
    return (gating * projected_out).astype(jnp.bfloat16)


def solution(mesh):
    placed = (P("row", ("col", "depth"), None), P(), P(), P(), P(), P(), P(), P())
    return jax.shard_map(
        per_device,
        mesh=mesh,
        in_specs=placed,
        out_specs=P("row", ("col", "depth"), None),
        check_vma=False,
    )
```

profile of v0, /device:TPU:0, one launch (start us, length us, event | category | flops | bytes accessed | tf_op | source)
XLA Modules:
  0.0 87.3 jit_solution(1574282504677348500)
XLA Ops:
  0.0 1.2 %convert_reduce_fusion = f32[48,24]{1,0:T(8,128)S(1)} fusion(bf16[48,24,128]{2,1,0:T(8,128)(2,1)} %param.8), kind=kLoop, calls=%fused_computation.18 | loop fusion | flops 293760 | bytes 299520 | tf_op jit(solution)/shard_map/reduce_sum | solution.py:8
  1.2 0.1 copy.85
  1.3 0.1 copy.86
  1.4 1.4 %fusion.15 = f32[48,24]{1,0:T(8,128)S(1)} fusion(bf16[48,24,128]{2,1,0:T(8,128)(2,1)} %param.8, f32[48,24]{1,0:T(8,128)S(1)} %copy.86), kind=kLoop, calls=%fused_computation.21 | loop fusion | flops 588672 | bytes 304128 | tf_op jit(solution)/shard_map/reduce_sum | solution.py:10
  2.8 0.1 copy.87
  2.8 0.1 copy.88
  2.9 1.6 %fusion.27 = f32[48,24,512]{2,1,0:T(8,128)S(1)} fusion(bf16[128,512]{1,0:T(8,128)(2,1)S(1)} %copy-done, bf16[48,24,128]{2,1,0:T(8,128)(2,1)} %param.8, f32[128]{0:T(128)} %param.10, f32[128]{0:T(128)} %param.9, f32[48,24]{1,0:T(8,128)S(1)} %copy.88, f32[48,24]{1,0:T(8,128)S(1)} %copy.86), kind=kOutput, calls=%fused_computation.37 | convolution fusion | flops 151879680 | bytes 2795520 | tf_op jit(solution)/shard_map/xyc,cd->xyd/dot_general | solution.py:16
  4.5 0.3 fusion.19
  4.8 0.5 copy.94
  5.3 2.0 %reshape.59 = bf16[4,2,18432]{2,1,0:T(2,128)(2,1)} reshape(bf16[128,24,48]{2,1,0:T(8,128)(2,1)S(1)} %bitcast.78) | data formatting | bytes 589824
  7.3 6.3 %all-to-all-start.2 = ((bf16[4,2,18432]{2,1,0:T(2,128)(2,1)}), bf16[4,2,18432]{2,1,0:T(2,128)(2,1)S(1)}, u32[]{:S(2)}, u32[]{:S(2)}) async-start(bf16[4,2,18432]{2,1,0:T(2,128)(2,1)} %reshape.59), calls=%async_computation.2 | async-start | bytes 589824 | tf_op jit(solution)/shard_map/all_to_all | solution.py:40
  13.7 0.5 copy.89
  14.1 2.0 %reshape.57 = bf16[4,2,18432]{2,1,0:T(2,128)(2,1)} reshape(bf16[128,24,48]{2,1,0:T(8,128)(2,1)S(1)} %bitcast.79) | data formatting | bytes 589824
  16.2 7.1 %all-to-all-done.2 = bf16[4,2,18432]{2,1,0:T(2,128)(2,1)S(1)} async-done(((bf16[4,2,18432]{2,1,0:T(2,128)(2,1)}), bf16[4,2,18432]{2,1,0:T(2,128)(2,1)S(1)}, u32[]{:S(2)}, u32[]{:S(2)}) %all-to-all-start.2) | async-done | bytes 294944 | tf_op jit(solution)/shard_map/all_to_all | solution.py:40
  23.3 3.5 %all-to-all-start = ((bf16[4,2,18432]{2,1,0:T(2,128)(2,1)}), bf16[4,2,18432]{2,1,0:T(2,128)(2,1)S(1)}, u32[]{:S(2)}, u32[]{:S(2)}) async-start(bf16[4,2,18432]{2,1,0:T(2,128)(2,1)} %reshape.57), calls=%async_computation | async-start | bytes 589824 | tf_op jit(solution)/shard_map/all_to_all | solution.py:47
  26.7 0.8 reshape.60
  27.5 0.6 copy.115
  28.1 1.2 %reshape.56 = bf16[192,24,32]{0,1,2:T(8,128)(2,1)} reshape(bf16[4,48,24,32]{1,0,2,3:T(4,128)(2,1)S(1)} %copy.115) | data formatting | bytes 589824 | tf_op jit(solution)/shard_map/all_to_all | solution.py:40
  29.3 5.5 %all-to-all-done = bf16[4,2,18432]{2,1,0:T(2,128)(2,1)S(1)} async-done(((bf16[4,2,18432]{2,1,0:T(2,128)(2,1)}), bf16[4,2,18432]{2,1,0:T(2,128)(2,1)S(1)}, u32[]{:S(2)}, u32[]{:S(2)}) %all-to-all-start) | async-done | bytes 294944 | tf_op jit(solution)/shard_map/all_to_all | solution.py:47
  34.9 3.7 %all-to-all-start.3 = ((bf16[192,24,32]{0,1,2:T(8,128)(2,1)}), bf16[192,24,32]{0,1,2:T(8,128)(2,1)S(1)}, u32[]{:S(2)}, u32[]{:S(2)}) async-start(bf16[192,24,32]{0,1,2:T(8,128)(2,1)} %reshape.56), calls=%async_computation.3 | async-start | bytes 786432 | tf_op jit(solution)/shard_map/all_to_all | solution.py:39
  38.6 0.8 reshape.58
  39.4 0.6 copy.113
  40.0 1.2 %reshape.55 = bf16[192,24,32]{0,1,2:T(8,128)(2,1)} reshape(bf16[4,48,24,32]{1,0,2,3:T(4,128)(2,1)S(1)} %copy.113) | data formatting | bytes 589824 | tf_op jit(solution)/shard_map/all_to_all | solution.py:47
  41.2 4.9 %all-to-all-done.3 = bf16[192,24,32]{0,1,2:T(8,128)(2,1)S(1)} async-done(((bf16[192,24,32]{0,1,2:T(8,128)(2,1)}), bf16[192,24,32]{0,1,2:T(8,128)(2,1)S(1)}, u32[]{:S(2)}, u32[]{:S(2)}) %all-to-all-start.3) | async-done | bytes 294944 | tf_op jit(solution)/shard_map/all_to_all | solution.py:39
  46.0 3.5 %all-to-all-start.1 = ((bf16[192,24,32]{0,1,2:T(8,128)(2,1)}), bf16[192,24,32]{0,1,2:T(8,128)(2,1)S(1)}, u32[]{:S(2)}, u32[]{:S(2)}) async-start(bf16[192,24,32]{0,1,2:T(8,128)(2,1)} %reshape.55), calls=%async_computation.1 | async-start | bytes 786432 | tf_op jit(solution)/shard_map/all_to_all | solution.py:46
  49.5 7.3 %all-to-all-done.1 = bf16[192,24,32]{0,1,2:T(8,128)(2,1)S(1)} async-done(((bf16[192,24,32]{0,1,2:T(8,128)(2,1)}), bf16[192,24,32]{0,1,2:T(8,128)(2,1)S(1)}, u32[]{:S(2)}, u32[]{:S(2)}) %all-to-all-start.1) | async-done | bytes 294944 | tf_op jit(solution)/shard_map/all_to_all | solution.py:46
  56.9 0.3 fusion.12
  57.2 0.3 copy.100
  57.5 14.1 %all_to_all.99 = bf16[192,192,4]{1,2,0:T(4,128)(2,1)S(1)} all-to-all(bf16[192,192,4]{1,2,0:T(4,128)(2,1)S(1)} %copy.100), channel_id=1, replica_groups=mesh['row'=4,'col'=2,'depth'=4] {'row'}, dimensions={0} | all-to-all | bytes 589824 | tf_op jit(solution)/shard_map/all_to_all | solution.py:56
  71.7 0.0 copy-start.5
  71.8 0.7 copy.103
  72.4 1.9 %reshape.61 = bf16[8,2,9216]{2,1,0:T(2,128)(2,1)} reshape(bf16[192,16,48]{2,1,0:T(8,128)(2,1)S(1)} %bitcast.76) | data formatting | bytes 589824
  74.3 3.6 %all-to-all-start.5 = ((bf16[8,2,9216]{2,1,0:T(2,128)(2,1)}), bf16[8,2,9216]{2,1,0:T(2,128)(2,1)S(1)}, u32[]{:S(2)}, u32[]{:S(2)}) async-start(bf16[8,2,9216]{2,1,0:T(2,128)(2,1)} %reshape.61), calls=%async_computation.5 | async-start | bytes 589824 | tf_op jit(solution)/shard_map/all_to_all | solution.py:55
  77.9 0.1 reshape.47
  78.0 0.1 copy.104
  78.1 0.1 copy.105
  78.2 0.1 reshape.48
  78.3 0.1 copy.106
  78.4 0.1 copy.107
  78.6 0.5 fusion.10
  79.1 4.9 %all-to-all-done.5 = bf16[8,2,9216]{2,1,0:T(2,128)(2,1)S(1)} async-done(((bf16[8,2,9216]{2,1,0:T(2,128)(2,1)}), bf16[8,2,9216]{2,1,0:T(2,128)(2,1)S(1)}, u32[]{:S(2)}, u32[]{:S(2)}) %all-to-all-start.5) | async-done | bytes 294944 | tf_op jit(solution)/shard_map/all_to_all | solution.py:55
  84.1 0.8 reshape.62
  84.8 0.2 fusion.1
  85.0 0.3 fusion.4
  85.3 0.4 fusion.7
  85.7 0.2 copy.108
  86.0 0.3 copy.110
  86.3 1.0 %fusion.11 = bf16[48,24,128]{2,1,0:T(8,128)(2,1)} fusion(f32[48,24,128]{2,1,0:T(8,128)S(1)} %fusion.10, bf16[48,24,128]{2,1,0:T(8,128)(2,1)S(1)} %copy.110, bf16[128,128,1]{1,0,2:T(8,128)(2,1)S(1)} %bitcast.86), kind=kOutput, calls=%fused_computation.15 | convolution fusion | flops 38043648 | bytes 1212416 | tf_op jit(solution)/shard_map/xyc,cd->xyd/dot_general | solution.py:70
  (24 shorter events, 0.2 us)
Async XLA Ops:
  0.0 2.9 %copy-start = (bf16[128,512]{1,0:T(8,128)(2,1)S(1)}, bf16[128,512]{1,0:T(8,128)(2,1)}, u32[]{:S(2)}) copy-start(bf16[128,512]{1,0:T(8,128)(2,1)} %param.11) | copy-start | bytes 393220
  7.3 16.0 %all-to-all-start.2 = ((bf16[4,2,18432]{2,1,0:T(2,128)(2,1)}), bf16[4,2,18432]{2,1,0:T(2,128)(2,1)S(1)}, u32[]{:S(2)}, u32[]{:S(2)}) async-start(bf16[4,2,18432]{2,1,0:T(2,128)(2,1)} %reshape.59), calls=%async_computation.2 | async-start | bytes 589824 | tf_op jit(solution)/shard_map/all_to_all | solution.py:40
  23.3 11.6 %all-to-all-start = ((bf16[4,2,18432]{2,1,0:T(2,128)(2,1)}), bf16[4,2,18432]{2,1,0:T(2,128)(2,1)S(1)}, u32[]{:S(2)}, u32[]{:S(2)}) async-start(bf16[4,2,18432]{2,1,0:T(2,128)(2,1)} %reshape.57), calls=%async_computation | async-start | bytes 589824 | tf_op jit(solution)/shard_map/all_to_all | solution.py:47
  34.9 11.2 %all-to-all-start.3 = ((bf16[192,24,32]{0,1,2:T(8,128)(2,1)}), bf16[192,24,32]{0,1,2:T(8,128)(2,1)S(1)}, u32[]{:S(2)}, u32[]{:S(2)}) async-start(bf16[192,24,32]{0,1,2:T(8,128)(2,1)} %reshape.56), calls=%async_computation.3 | async-start | bytes 786432 | tf_op jit(solution)/shard_map/all_to_all | solution.py:39
  46.0 10.8 %all-to-all-start.1 = ((bf16[192,24,32]{0,1,2:T(8,128)(2,1)}), bf16[192,24,32]{0,1,2:T(8,128)(2,1)S(1)}, u32[]{:S(2)}, u32[]{:S(2)}) async-start(bf16[192,24,32]{0,1,2:T(8,128)(2,1)} %reshape.55), calls=%async_computation.1 | async-start | bytes 786432 | tf_op jit(solution)/shard_map/all_to_all | solution.py:46
  71.7 6.3 %copy-start.5 = (f32[128]{0:T(128)S(1)}, f32[128]{0:T(128)}, u32[]{:S(2)}) copy-start(f32[128]{0:T(128)} %param.13) | copy-start | bytes 1540
  71.7 6.5 %copy-start.6 = (f32[128]{0:T(128)S(1)}, f32[128]{0:T(128)}, u32[]{:S(2)}) copy-start(f32[128]{0:T(128)} %param.14) | copy-start | bytes 1540
  71.7 6.8 %copy-start.2 = (bf16[128,128]{1,0:T(8,128)(2,1)S(1)}, bf16[128,128]{1,0:T(8,128)(2,1)}, u32[]{:S(2)}) copy-start(bf16[128,128]{1,0:T(8,128)(2,1)} %param.15) | copy-start | bytes 98308
  71.7 6.8 %copy-start.1 = (bf16[48,24,128]{2,1,0:T(8,128)(2,1)S(1)}, bf16[48,24,128]{2,1,0:T(8,128)(2,1)}, u32[]{:S(2)}) copy-start(bf16[48,24,128]{2,1,0:T(8,128)(2,1)} %param.8) | copy-start | bytes 884740
  71.7 6.8 %copy-start.3 = (f32[128]{0:T(128)S(1)}, f32[128]{0:T(128)}, u32[]{:S(2)}) copy-start(f32[128]{0:T(128)} %param.10) | copy-start | bytes 1540
  71.7 6.8 %copy-start.4 = (f32[128]{0:T(128)S(1)}, f32[128]{0:T(128)}, u32[]{:S(2)}) copy-start(f32[128]{0:T(128)} %param.9) | copy-start | bytes 1540
  71.7 6.8 %copy-start.7 = (bf16[128,128]{1,0:T(8,128)(2,1)S(1)}, bf16[128,128]{1,0:T(8,128)(2,1)}, u32[]{:S(2)}) copy-start(bf16[128,128]{1,0:T(8,128)(2,1)} %param.12) | copy-start | bytes 98308
  74.3 9.7 %all-to-all-start.5 = ((bf16[8,2,9216]{2,1,0:T(2,128)(2,1)}), bf16[8,2,9216]{2,1,0:T(2,128)(2,1)S(1)}, u32[]{:S(2)}, u32[]{:S(2)}) async-start(bf16[8,2,9216]{2,1,0:T(2,128)(2,1)} %reshape.61), calls=%async_computation.5 | async-start | bytes 589824 | tf_op jit(solution)/shard_map/all_to_all | solution.py:55
where the time goes:
time: 88 us; the launch traced here: 87.3 us
  waiting for transfers between devices  29.8 us (34%)
  starting transfers between devices  20.6 us (23%)
  local copies, waits for them, and re-layouts  15.3 us (17%)
  blocking collectives  14.1 us (16%)
  other arithmetic  3.81 us (4%)
  matrix products  3.41 us (4%)
    all_to_all x1, blocking collectives, per_device(): lax.all_to_all(planes.astype(jnp.bfloat16), 'row', split_axis=0, concat_a...  14.1 us
    unnamed x22, local copies, waits for them, and re-layouts  8.3 us
    all_to_all x1, waiting for transfers between devices, per_device(): lax.all_to_all(lax.all_to_all(right_side, 'row', split_axis=2, concat_axi...  7.34 us
    all_to_all x1, waiting for transfers between devices, per_device(): lax.all_to_all(left_side, 'row', split_axis=2, concat_axis=0, tiled=True)  7.1 us
    all_to_all x1, starting transfers between devices, per_device(): lax.all_to_all(left_side, 'row', split_axis=2, concat_axis=0, tiled=True)  6.35 us
    all_to_all x1, waiting for transfers between devices, per_device(): lax.all_to_all(right_side, 'row', split_axis=2, concat_axis=0, tiled=True)  5.54 us
    all_to_all x1, waiting for transfers between devices, per_device(): lax.all_to_all(lax.all_to_all(planes.astype(jnp.bfloat16), 'row', split_a...  4.94 us
    all_to_all x1, waiting for transfers between devices, per_device(): lax.all_to_all(lax.all_to_all(left_side, 'row', split_axis=2, concat_axis...  4.88 us
  transfers between devices with their start and end apart: 5, of which 5 were waited for; matrix products, arithmetic and copies ran while one was open for 10% of the time, Pallas kernels for 0%

commit v1 on v0

--- a/solution.py
+++ b/solution.py
@@ -44,7 +44,12 @@
             tiled=True,
         ),
         lax.all_to_all(
-            lax.all_to_all(right_side, "row", split_axis=2, concat_axis=0, tiled=True),
+            jnp.concatenate(
+                lax.all_to_all(
+                    jnp.stack(jnp.split(right_side, lax.axis_size("row"), axis=2)), "row", 0, 0
+                ),
+                axis=0,
+            ),
             ("col", "depth"),
             split_axis=2,
             concat_axis=1,

time: 88 us -> 88.9 us (1.010)
    all_to_all x2, starting transfers between devices: 6.9 us -> 10.1 us  [the longest x1 6.35 us: per_device(): lax.all_to_all(jnp.stack(jnp.split(right_side, lax.axis_size('row'), axis...]
    all_to_all x1, starting transfers between devices: 6.35 us -> 3.45 us  [per_device(): lax.all_to_all(left_side, 'row', split_axis=2, concat_axis=0, tiled=True)]
    all_to_all x1, waiting for transfers between devices: 4.88 us -> 7.34 us  [per_device(): lax.all_to_all(lax.all_to_all(left_side, 'row', split_axis=2, concat_axis...]
    all_to_all x1, waiting for transfers between devices: 7.1 us -> 5.56 us  [per_device(): lax.all_to_all(left_side, 'row', split_axis=2, concat_axis=0, tiled=True)]
    all_to_all x3 -> x2, local copies, waits for them, and re-layouts: 1.81 us -> 0.64 us  [the longest x1 0.61 us: per_device(): lax.all_to_all(jnp.stack(jnp.split(right_side, lax.axis_size('row'), axis...]
    reshape x0 -> x1, local copies, waits for them, and re-layouts: none -> 1.17 us  [per_device(): jnp.concatenate(lax.all_to_all(jnp.stack(jnp.split(right_side, lax.axis_s...]
    another operation x0 -> x2, local copies, waits for them, and re-layouts: none -> 1.08 us  [per_device(): jnp.stack(jnp.split(right_side, lax.axis_size('row'), axis=2))]
    all_to_all x2, waiting for transfers between devices: 12.9 us -> 12 us  [the longest x1 7.1 us: per_device(): lax.all_to_all(jnp.stack(jnp.split(right_side, lax.axis_size('row'), axis...]
where the time goes in v1:
time: 88.9 us; the launch traced here: 88.2 us
  waiting for transfers between devices  30 us (34%)
  starting transfers between devices  20.4 us (23%)
  local copies, waits for them, and re-layouts  15.9 us (18%)
  blocking collectives  14.1 us (16%)
  other arithmetic  4.12 us (5%)
  matrix products  3.42 us (4%)
    all_to_all x1, blocking collectives, per_device(): lax.all_to_all(planes.astype(jnp.bfloat16), 'row', split_axis=0, concat_a...  14.1 us
    unnamed x22, local copies, waits for them, and re-layouts  8.3 us
    all_to_all x1, waiting for transfers between devices, per_device(): lax.all_to_all(lax.all_to_all(left_side, 'row', split_axis=2, concat_axis...  7.34 us
    all_to_all x1, waiting for transfers between devices, per_device(): lax.all_to_all(jnp.stack(jnp.split(right_side, lax.axis_size('row'), axis...  7.1 us
    all_to_all x1, starting transfers between devices, per_device(): lax.all_to_all(jnp.stack(jnp.split(right_side, lax.axis_size('row'), axis...  6.35 us
    all_to_all x1, waiting for transfers between devices, per_device(): lax.all_to_all(left_side, 'row', split_axis=2, concat_axis=0, tiled=True)  5.56 us
    all_to_all x1, waiting for transfers between devices, per_device(): lax.all_to_all(lax.all_to_all(planes.astype(jnp.bfloat16), 'row', split_a...  5.12 us
    all_to_all x1, waiting for transfers between devices, per_device(): lax.all_to_all(jnp.concatenate(lax.all_to_all(jnp.stack(jnp.split(right_s...  4.87 us
  transfers between devices with their start and end apart: 5, of which 5 were waited for; matrix products, arithmetic and copies ran while one was open for 10% of the time, Pallas kernels for 0%

profile of v1, /device:TPU:0, one launch (start us, length us, event | category | flops | bytes accessed | tf_op | source)
XLA Modules:
  0.0 88.2 jit_solution(6928074093538055693)
XLA Ops:
  0.0 1.2 %convert_reduce_fusion = f32[48,24]{1,0:T(8,128)S(1)} fusion(bf16[48,24,128]{2,1,0:T(8,128)(2,1)} %param.8), kind=kLoop, calls=%fused_computation.19 | loop fusion | flops 293760 | bytes 299520 | tf_op jit(solution)/shard_map/reduce_sum | solution.py:8
  1.2 0.1 copy.80
  1.3 0.1 copy.81
  1.4 1.4 %fusion.15 = f32[48,24]{1,0:T(8,128)S(1)} fusion(bf16[48,24,128]{2,1,0:T(8,128)(2,1)} %param.8, f32[48,24]{1,0:T(8,128)S(1)} %copy.81), kind=kLoop, calls=%fused_computation.22 | loop fusion | flops 588672 | bytes 304128 | tf_op jit(solution)/shard_map/reduce_sum | solution.py:10
  2.8 0.1 copy.83
  2.9 1.6 %fusion.27 = f32[48,24,512]{2,1,0:T(8,128)S(1)} fusion(bf16[128,512]{1,0:T(8,128)(2,1)S(1)} %copy-done, bf16[48,24,128]{2,1,0:T(8,128)(2,1)} %param.8, f32[128]{0:T(128)} %param.10, f32[128]{0:T(128)} %param.9, f32[48,24]{1,0:T(8,128)S(1)} %copy.83, f32[48,24]{1,0:T(8,128)S(1)} %copy.81), kind=kOutput, calls=%fused_computation.42 | convolution fusion | flops 151879680 | bytes 2795520 | tf_op jit(solution)/shard_map/xyc,cd->xyd/dot_general | solution.py:16
  4.5 0.3 fusion.19
  4.8 0.3 slice_bitcast_fusion.3
  5.1 0.3 pad_maximum_fusion
  5.4 0.8 copy.84
  6.2 2.0 %reshape.60 = bf16[4,2,18432]{2,1,0:T(2,128)(2,1)} reshape(bf16[4,24,32,48]{3,2,1,0:T(8,128)(2,1)S(1)} %bitcast.84) | data formatting | bytes 589824
  8.2 6.3 %all-to-all-start = ((bf16[4,2,18432]{2,1,0:T(2,128)(2,1)}), bf16[4,2,18432]{2,1,0:T(2,128)(2,1)S(1)}, u32[]{:S(2)}, u32[]{:S(2)}) async-start(bf16[4,2,18432]{2,1,0:T(2,128)(2,1)} %reshape.60), calls=%async_computation | async-start | bytes 589824 | tf_op jit(solution)/shard_map/all_to_all | solution.py:48
  14.6 0.5 copy.87
  15.1 2.0 %reshape.62 = bf16[4,2,18432]{2,1,0:T(2,128)(2,1)} reshape(bf16[128,24,48]{2,1,0:T(8,128)(2,1)S(1)} %bitcast.83) | data formatting | bytes 589824
  17.1 7.1 %all-to-all-done = bf16[4,2,18432]{2,1,0:T(2,128)(2,1)S(1)} async-done(((bf16[4,2,18432]{2,1,0:T(2,128)(2,1)}), bf16[4,2,18432]{2,1,0:T(2,128)(2,1)S(1)}, u32[]{:S(2)}, u32[]{:S(2)}) %all-to-all-start) | async-done | bytes 294944 | tf_op jit(solution)/shard_map/all_to_all | solution.py:48
  24.2 3.5 %all-to-all-start.2 = ((bf16[4,2,18432]{2,1,0:T(2,128)(2,1)}), bf16[4,2,18432]{2,1,0:T(2,128)(2,1)S(1)}, u32[]{:S(2)}, u32[]{:S(2)}) async-start(bf16[4,2,18432]{2,1,0:T(2,128)(2,1)} %reshape.62), calls=%async_computation.2 | async-start | bytes 589824 | tf_op jit(solution)/shard_map/all_to_all | solution.py:40
  27.7 0.8 reshape.61
  28.4 0.6 copy.85
  29.1 1.2 %reshape.50 = bf16[192,24,32]{0,1,2:T(8,128)(2,1)} reshape(bf16[4,48,24,32]{1,0,2,3:T(4,128)(2,1)S(1)} %copy.85) | data formatting | bytes 589824 | tf_op jit(solution)/shard_map/reshape | solution.py:47
  30.2 5.6 %all-to-all-done.2 = bf16[4,2,18432]{2,1,0:T(2,128)(2,1)S(1)} async-done(((bf16[4,2,18432]{2,1,0:T(2,128)(2,1)}), bf16[4,2,18432]{2,1,0:T(2,128)(2,1)S(1)}, u32[]{:S(2)}, u32[]{:S(2)}) %all-to-all-start.2) | async-done | bytes 294944 | tf_op jit(solution)/shard_map/all_to_all | solution.py:40
  35.8 3.7 %all-to-all-start.1 = ((bf16[192,24,32]{0,1,2:T(8,128)(2,1)}), bf16[192,24,32]{0,1,2:T(8,128)(2,1)S(1)}, u32[]{:S(2)}, u32[]{:S(2)}) async-start(bf16[192,24,32]{0,1,2:T(8,128)(2,1)} %reshape.50), calls=%async_computation.1 | async-start | bytes 786432 | tf_op jit(solution)/shard_map/all_to_all | solution.py:46
  39.5 0.8 reshape.63
  40.3 0.6 copy.106
  40.9 1.2 %reshape.59 = bf16[192,24,32]{0,1,2:T(8,128)(2,1)} reshape(bf16[4,48,24,32]{1,0,2,3:T(4,128)(2,1)S(1)} %copy.106) | data formatting | bytes 589824 | tf_op jit(solution)/shard_map/all_to_all | solution.py:40
  42.1 4.9 %all-to-all-done.1 = bf16[192,24,32]{0,1,2:T(8,128)(2,1)S(1)} async-done(((bf16[192,24,32]{0,1,2:T(8,128)(2,1)}), bf16[192,24,32]{0,1,2:T(8,128)(2,1)S(1)}, u32[]{:S(2)}, u32[]{:S(2)}) %all-to-all-start.1) | async-done | bytes 294944 | tf_op jit(solution)/shard_map/all_to_all | solution.py:46
  47.0 3.5 %all-to-all-start.3 = ((bf16[192,24,32]{0,1,2:T(8,128)(2,1)}), bf16[192,24,32]{0,1,2:T(8,128)(2,1)S(1)}, u32[]{:S(2)}, u32[]{:S(2)}) async-start(bf16[192,24,32]{0,1,2:T(8,128)(2,1)} %reshape.59), calls=%async_computation.3 | async-start | bytes 786432 | tf_op jit(solution)/shard_map/all_to_all | solution.py:39
  50.5 7.3 %all-to-all-done.3 = bf16[192,24,32]{0,1,2:T(8,128)(2,1)S(1)} async-done(((bf16[192,24,32]{0,1,2:T(8,128)(2,1)}), bf16[192,24,32]{0,1,2:T(8,128)(2,1)S(1)}, u32[]{:S(2)}, u32[]{:S(2)}) %all-to-all-start.3) | async-done | bytes 294944 | tf_op jit(solution)/shard_map/all_to_all | solution.py:39
  57.8 0.3 fusion.12
  58.1 0.3 copy.93
  58.4 14.1 %all_to_all.86 = bf16[192,192,4]{1,2,0:T(4,128)(2,1)S(1)} all-to-all(bf16[192,192,4]{1,2,0:T(4,128)(2,1)S(1)} %copy.93), channel_id=1, replica_groups=mesh['row'=4,'col'=2,'depth'=4] {'row'}, dimensions={0} | all-to-all | bytes 589824 | tf_op jit(solution)/shard_map/all_to_all | solution.py:61
  72.7 0.7 copy.96
  73.4 1.9 %reshape.64 = bf16[8,2,9216]{2,1,0:T(2,128)(2,1)} reshape(bf16[192,16,48]{2,1,0:T(8,128)(2,1)S(1)} %bitcast.81) | data formatting | bytes 589824
  75.2 3.4 %all-to-all-start.5 = ((bf16[8,2,9216]{2,1,0:T(2,128)(2,1)}), bf16[8,2,9216]{2,1,0:T(2,128)(2,1)S(1)}, u32[]{:S(2)}, u32[]{:S(2)}) async-start(bf16[8,2,9216]{2,1,0:T(2,128)(2,1)} %reshape.64), calls=%async_computation.5 | async-start | bytes 589824 | tf_op jit(solution)/shard_map/all_to_all | solution.py:60
  78.7 0.1 reshape.52
  78.8 0.1 copy.99
  78.9 0.1 copy.100
  79.0 0.1 reshape.51
  79.1 0.1 copy.97
  79.2 0.1 copy.98
  79.3 0.5 fusion.10
  79.9 5.1 %all-to-all-done.5 = bf16[8,2,9216]{2,1,0:T(2,128)(2,1)S(1)} async-done(((bf16[8,2,9216]{2,1,0:T(2,128)(2,1)}), bf16[8,2,9216]{2,1,0:T(2,128)(2,1)S(1)}, u32[]{:S(2)}, u32[]{:S(2)}) %all-to-all-start.5) | async-done | bytes 294944 | tf_op jit(solution)/shard_map/all_to_all | solution.py:60
  85.0 0.8 reshape.65
  85.8 0.2 fusion.1
  86.0 0.3 fusion.4
  86.3 0.4 fusion.7
  86.7 0.2 copy.101
  86.9 0.3 copy.103
  87.2 1.0 %fusion.11 = bf16[48,24,128]{2,1,0:T(8,128)(2,1)} fusion(f32[48,24,128]{2,1,0:T(8,128)S(1)} %fusion.10, bf16[48,24,128]{2,1,0:T(8,128)(2,1)S(1)} %copy.103, bf16[128,128,1]{1,0,2:T(8,128)(2,1)S(1)} %bitcast.91), kind=kOutput, calls=%fused_computation.15 | convolution fusion | flops 38043648 | bytes 1212416 | tf_op jit(solution)/shard_map/xyc,cd->xyd/dot_general | solution.py:75
  (26 shorter events, 0.3 us)
Async XLA Ops:
  0.0 2.9 %copy-start = (bf16[128,512]{1,0:T(8,128)(2,1)S(1)}, bf16[128,512]{1,0:T(8,128)(2,1)}, u32[]{:S(2)}) copy-start(bf16[128,512]{1,0:T(8,128)(2,1)} %param.11) | copy-start | bytes 393220
  8.2 16.0 %all-to-all-start = ((bf16[4,2,18432]{2,1,0:T(2,128)(2,1)}), bf16[4,2,18432]{2,1,0:T(2,128)(2,1)S(1)}, u32[]{:S(2)}, u32[]{:S(2)}) async-start(bf16[4,2,18432]{2,1,0:T(2,128)(2,1)} %reshape.60), calls=%async_computation | async-start | bytes 589824 | tf_op jit(solution)/shard_map/all_to_all | solution.py:48
  24.2 11.6 %all-to-all-start.2 = ((bf16[4,2,18432]{2,1,0:T(2,128)(2,1)}), bf16[4,2,18432]{2,1,0:T(2,128)(2,1)S(1)}, u32[]{:S(2)}, u32[]{:S(2)}) async-start(bf16[4,2,18432]{2,1,0:T(2,128)(2,1)} %reshape.62), calls=%async_computation.2 | async-start | bytes 589824 | tf_op jit(solution)/shard_map/all_to_all | solution.py:40
  35.8 11.2 %all-to-all-start.1 = ((bf16[192,24,32]{0,1,2:T(8,128)(2,1)}), bf16[192,24,32]{0,1,2:T(8,128)(2,1)S(1)}, u32[]{:S(2)}, u32[]{:S(2)}) async-start(bf16[192,24,32]{0,1,2:T(8,128)(2,1)} %reshape.50), calls=%async_computation.1 | async-start | bytes 786432 | tf_op jit(solution)/shard_map/all_to_all | solution.py:46
  47.0 10.8 %all-to-all-start.3 = ((bf16[192,24,32]{0,1,2:T(8,128)(2,1)}), bf16[192,24,32]{0,1,2:T(8,128)(2,1)S(1)}, u32[]{:S(2)}, u32[]{:S(2)}) async-start(bf16[192,24,32]{0,1,2:T(8,128)(2,1)} %reshape.59), calls=%async_computation.3 | async-start | bytes 786432 | tf_op jit(solution)/shard_map/all_to_all | solution.py:39
  72.6 6.1 %copy-start.5 = (f32[128]{0:T(128)S(1)}, f32[128]{0:T(128)}, u32[]{:S(2)}) copy-start(f32[128]{0:T(128)} %param.14) | copy-start | bytes 1540
  72.6 6.3 %copy-start.6 = (f32[128]{0:T(128)S(1)}, f32[128]{0:T(128)}, u32[]{:S(2)}) copy-start(f32[128]{0:T(128)} %param.13) | copy-start | bytes 1540
  72.6 6.6 %copy-start.2 = (bf16[128,128]{1,0:T(8,128)(2,1)S(1)}, bf16[128,128]{1,0:T(8,128)(2,1)}, u32[]{:S(2)}) copy-start(bf16[128,128]{1,0:T(8,128)(2,1)} %param.15) | copy-start | bytes 98308
  72.6 6.6 %copy-start.1 = (bf16[48,24,128]{2,1,0:T(8,128)(2,1)S(1)}, bf16[48,24,128]{2,1,0:T(8,128)(2,1)}, u32[]{:S(2)}) copy-start(bf16[48,24,128]{2,1,0:T(8,128)(2,1)} %param.8) | copy-start | bytes 884740
  72.6 6.6 %copy-start.3 = (f32[128]{0:T(128)S(1)}, f32[128]{0:T(128)}, u32[]{:S(2)}) copy-start(f32[128]{0:T(128)} %param.10) | copy-start | bytes 1540
  72.7 6.6 %copy-start.4 = (f32[128]{0:T(128)S(1)}, f32[128]{0:T(128)}, u32[]{:S(2)}) copy-start(f32[128]{0:T(128)} %param.9) | copy-start | bytes 1540
  72.7 6.6 %copy-start.7 = (bf16[128,128]{1,0:T(8,128)(2,1)S(1)}, bf16[128,128]{1,0:T(8,128)(2,1)}, u32[]{:S(2)}) copy-start(bf16[128,128]{1,0:T(8,128)(2,1)} %param.12) | copy-start | bytes 98308
  75.2 9.7 %all-to-all-start.5 = ((bf16[8,2,9216]{2,1,0:T(2,128)(2,1)}), bf16[8,2,9216]{2,1,0:T(2,128)(2,1)S(1)}, u32[]{:S(2)}, u32[]{:S(2)}) async-start(bf16[8,2,9216]{2,1,0:T(2,128)(2,1)} %reshape.64), calls=%async_computation.5 | async-start | bytes 589824 | tf_op jit(solution)/shard_map/all_to_all | solution.py:60
